TPU v7x, 32 devices: a whole 2x2x4 slice. The times are simulated.
32 devices in a mesh: pp: 4 (over x, core), tp: 2 (over y), dp: 4 (over z).
Axes of the slice: x: 2, y: 2, z: 4, core: 2. Of those that a mesh axis runs over, the one named last changes fastest.
Arguments:
- layer_input: bfloat16 [4, 4, 16, 4096], P('pp', 'dp', 'tp'), may hold values from -4 to 4
- gate_pre: bfloat16 [4, 4, 16, 14784], P('pp', 'dp', None, 'tp'), may hold values from -8 to 8
- up_pre: bfloat16 [4, 4, 16, 14784], P('pp', 'dp', None, 'tp'), may hold values from -6 to 6
- hidden_grad: bfloat16 [4, 4, 16, 14784], P('pp', 'dp', None, 'tp'), may hold values from -0.59765625 to 0.59765625
- gate_weight: bfloat16 [4, 4096, 14784], P('pp', 'dp', 'tp'), may hold values from -0.09375 to 0.09375
Outputs:
- passed_grad: bfloat16 [4, 4, 16, 4096], P('pp', 'dp', 'tp')
- gate_weight_grad: bfloat16 [4, 4096, 14784], P('pp', 'dp', 'tp')
All inputs are finite; a program needn't handle non-finite values.
Results may differ from a plain program's by a relative error of at most 0.018.
Values may be sent and summed in bfloat16 or wider, within the bound.
No kernel may reach another device: no remote copies, remote signals or barrier semaphores. Data moves between devices by JAX's collectives and lax.ppermute only.
A program may use at most 128 MiB of HBM per device.

v0:
```python
import jax
import jax.numpy as jnp
from jax import lax
from jax.sharding import PartitionSpec as P


def from_behind(block, axis, distance):
    devices = range(lax.axis_size(axis))
    route = [(i - distance, i) for i in devices if i - distance in devices]
    return lax.ppermute(block, axis, route)


def finish(partial_value):
    return lax.psum_scatter(
        partial_value.astype(jnp.bfloat16), "tp", scatter_dimension=0, tiled=True
    )


def on_device(layer_input, gate_pre, up_pre, hidden_grad, gate_weight):
    tokens_in = layer_input[0, 0]
    gate_val = gate_pre[0, 0].astype(jnp.float32)
    up_val = up_pre[0, 0].astype(jnp.float32)
    hidden_val = hidden_grad[0, 0].astype(jnp.float32)
    gate_local = gate_weight[0]
    rows_total = gate_val.shape[0]
    groups = lax.axis_size("dp")
    logistic = jax.nn.sigmoid(gate_val)
    gate_grad = (hidden_val * up_val * logistic * (1.0 + gate_val * (1.0 - logistic))).astype(
        jnp.bfloat16
    )
    gathered_in = lax.all_gather(tokens_in, "tp", axis=0, tiled=True)
    contract_cols = (((1,), (1,)), ((), ()))
    all_grads = lax.all_gather(gate_grad, "dp", axis=0, tiled=True)
    partial_value = lax.dot_general(
        all_grads, gate_local, contract_cols, preferred_element_type=jnp.float32
    )
    returned = lax.all_to_all(
        partial_value.astype(jnp.bfloat16), "dp", split_axis=0, concat_axis=1, tiled=True
    ).astype(partial_value.dtype)
    input_grad = finish(returned)
    in_columns = lax.all_to_all(gathered_in, "dp", split_axis=1, concat_axis=0, tiled=True)
    products = lax.dot_general(
        in_columns.reshape(groups, rows_total, in_columns.shape[1]),
        all_grads.reshape(groups, rows_total, all_grads.shape[1]),
        (((1,), (1,)), ((0,), (0,))),
        preferred_element_type=jnp.float32,
    )
    rounded = lax.optimization_barrier(products.astype(jnp.bfloat16))
    grads_total = jnp.sum(rounded.astype(jnp.float32), axis=0)
    passed = from_behind(input_grad, "pp", -1)
    gate_out = grads_total.astype(jnp.bfloat16)
    return (passed[None, None], gate_out[None])


def solution(mesh):
    return jax.shard_map(
        on_device,
        mesh=mesh,
        in_specs=(
            P("pp", "dp", "tp", None),
            P("pp", "dp", None, "tp"),
            P("pp", "dp", None, "tp"),
            P("pp", "dp", None, "tp"),
            P("pp", "dp", "tp"),
        ),
        out_specs=(P("pp", "dp", "tp", None), P("pp", "dp", "tp")),
        check_vma=False,
    )
```

profile of v0, /device:TPU:0, one launch (start us, length us, event | category | flops | bytes accessed | tf_op | source)
XLA Modules:
  0.0 123.4 jit_solution(5903681675003052307)
XLA Ops:
  7.2 0.0 copy-start
  7.2 0.0 reduce-scatter.2.cloned.1.call-start
  7.2 1.4 %fusion.10 = bf16[16,7392]{1,0:T(8,128)(2,1)S(1)} fusion(bf16[1,1,16,7392]{3,2,1,0:T(8,128)(2,1)} %param.7, bf16[1,1,16,7392]{3,2,1,0:T(8,128)(2,1)} %param.8, bf16[1,1,16,7392]{3,2,1,0:T(8,128)(2,1)} %param.6), kind=kLoop, calls=%fused_computation.11 | loop fusion | flops 1537536 | bytes 946176 | tf_op jit(solution)/shard_map/convert_element_type | solution.py:28
  8.6 23.1 %all_gather.6 = bf16[64,7392]{1,0:T(8,128)(2,1)S(1)} all-gather(bf16[16,7392]{1,0:T(8,128)(2,1)S(1)} %fusion.10), channel_id=1, replica_groups=mesh['pp'=4,'tp'=2,'dp'=4] {'dp'}, dimensions={0}, use_global_device_ids=true | all-gather | bytes 1182720 | tf_op jit(solution)/shard_map/all_gather | solution.py:33
  31.7 8.0 %fusion.2 = bf16[64,1024]{1,0:T(8,128)(2,1)S(1)} fusion(bf16[64,7392]{1,0:T(8,128)(2,1)S(1)} %all_gather.6, bf16[1,1024,7392]{1,2,0:T(8,128)(2,1)} %param.9), kind=kOutput, calls=%fused_computation.3 | convolution fusion | flops 968949760 | bytes 16216064 | tf_op jit(solution)/shard_map/dot_general | solution.py:34
  39.8 9.1 %all_to_all.35 = bf16[4,16,1024]{2,1,0:T(8,128)(2,1)S(1)} all-to-all(bf16[4,16,1024]{2,1,0:T(8,128)(2,1)S(1)} %bitcast.30), channel_id=1, replica_groups=mesh['pp'=4,'tp'=2,'dp'=4] {'dp'}, dimensions={0} | all-to-all | bytes 262144 | tf_op jit(solution)/shard_map/all_to_all | solution.py:37
  48.9 0.7 copy.10
  49.5 0.0 reduce-scatter.2.cloned.1.call-update
  49.6 0.0 copy-done
  49.6 4.9 %all-gather = bf16[1,1,16,4096]{3,2,1,0:T(8,128)(2,1)S(1)} all-gather(bf16[1,1,8,4096]{3,2,1,0:T(8,128)(2,1)S(1)} %copy-done), channel_id=2, replica_groups=mesh['pp'=4,'tp'=2,'dp'=4] {'tp'}, dimensions={2}, use_global_device_ids=true | all-gather | bytes 196608 | tf_op jit(solution)/shard_map/all_gather | solution.py:31
  54.5 0.1 all_to_all.30
  54.6 0.7 copy.9
  55.3 3.3 %all-to-all-start.1 = ((bf16[16,4,1024]{2,0,1:T(8,128)(2,1)}), bf16[16,4,1024]{2,0,1:T(8,128)(2,1)S(1)}, u32[]{:S(2)}, u32[]{:S(2)}) async-start(bf16[16,4,1024]{2,0,1:T(8,128)(2,1)} %copy.9), calls=%async_computation.2 | async-start | bytes 262144 | tf_op jit(solution)/shard_map/all_to_all | solution.py:41
  58.6 0.5 reduce-scatter.2.cloned.1.call-done
  59.1 1.3 %collective-permute-start = (bf16[8,4096]{1,0:T(8,128)(2,1)}, bf16[8,4096]{1,0:T(8,128)(2,1)S(1)}, u32[]{:S(2)}, u32[]{:S(2)}) collective-permute-start(bf16[8,4096]{1,0:T(8,128)(2,1)} %reduce-scatter.2.cloned.1.call-done), channel_id=1, source_target_pairs={{8,0},{16,8},{24,16},{9,1},{17,9},{25,17},{10,2},{18,10},{26,18},{... | collective-permute-start | bytes 196616 | tf_op jit(solution)/shard_map/ppermute | solution.py:10
  60.4 4.1 %all-to-all-done.1 = bf16[16,4,1024]{2,0,1:T(8,128)(2,1)S(1)} async-done(((bf16[16,4,1024]{2,0,1:T(8,128)(2,1)}), bf16[16,4,1024]{2,0,1:T(8,128)(2,1)S(1)}, u32[]{:S(2)}, u32[]{:S(2)}) %all-to-all-start.1) | async-done | bytes 131104 | tf_op jit(solution)/shard_map/all_to_all | solution.py:41
  64.5 23.4 %convert_bitcast_fusion = bf16[4,1024,7392]{1,2,0:T(8,128)(2,1)} fusion(bf16[4,16,7392]{2,1,0:T(8,128)(2,1)S(1)} %bitcast.28, bf16[16,4,1024]{2,0,1:T(8,128)(2,1)S(1)} %all-to-all-done.1), kind=kOutput, calls=%fused_computation | convolution fusion | flops 999161856 | bytes 61632512 | tf_op jit(solution)/shard_map/dot_general | solution.py:42
  87.9 28.0 %reduce_sum.12 = bf16[1024,7392]{0,1:T(8,128)(2,1)} reduce(bf16[4,1024,7392]{1,2,0:T(8,128)(2,1)} %convert_bitcast_fusion, bf16[]{:T(256)} %constant.4.clone.1), dimensions={0}, to_apply=%region_1.0 | reduce | flops 22708224 | bytes 75694080 | tf_op jit(solution)/shard_map/reduce_sum | solution.py:49
  115.9 0.0 collective-permute-done
  115.9 0.6 copy.12
Async XLA Ops:
  7.2 42.4 %copy-start = (bf16[1,1,8,4096]{3,2,1,0:T(8,128)(2,1)S(1)}, bf16[1,1,8,4096]{3,2,1,0:T(8,128)(2,1)}, u32[]{:S(2)}) copy-start(bf16[1,1,8,4096]{3,2,1,0:T(8,128)(2,1)} %param.5) | copy-start | bytes 196612
  7.2 51.9 %reduce-scatter.2.cloned.1.call-start = ((), (), s32[]{:S(2)}) async-start(), calls=%async_computation.3 | async-start | bytes 196608 | tf_op jit(solution)/shard_map/reduce_scatter | solution.py:14
  55.3 9.2 %all-to-all-start.1 = ((bf16[16,4,1024]{2,0,1:T(8,128)(2,1)}), bf16[16,4,1024]{2,0,1:T(8,128)(2,1)S(1)}, u32[]{:S(2)}, u32[]{:S(2)}) async-start(bf16[16,4,1024]{2,0,1:T(8,128)(2,1)} %copy.9), calls=%async_computation.2 | async-start | bytes 262144 | tf_op jit(solution)/shard_map/all_to_all | solution.py:41
  59.1 56.8 %collective-permute-start = (bf16[8,4096]{1,0:T(8,128)(2,1)}, bf16[8,4096]{1,0:T(8,128)(2,1)S(1)}, u32[]{:S(2)}, u32[]{:S(2)}) collective-permute-start(bf16[8,4096]{1,0:T(8,128)(2,1)} %reduce-scatter.2.cloned.1.call-done), channel_id=1, source_target_pairs={{8,0},{16,8},{24,16},{9,1},{17,9},{25,17},{10,2},{18,10},{26,18},{... | collective-permute-start | bytes 196616 | tf_op jit(solution)/shard_map/ppermute | solution.py:10
Sparse Core Ops, SparseCore 0:
  49.7 9.3 reduce-scatter.1
where the time goes:
time: 124 us; the launch traced here: 123 us
  blocking collectives  37.1 us (30%)
  matrix products  31.5 us (25%)
  other arithmetic  29.4 us (24%)
  between operations  14.1 us (11%)
  starting transfers between devices  4.64 us (4%)
  waiting for transfers between devices  4.62 us (4%)
  local copies, waits for them, and re-layouts  2.05 us (2%)
    reduce_sum x1, other arithmetic, on_device(): grads_total = jnp.sum(rounded.astype(jnp.float32), axis=0)  28 us
    dot_general x1, matrix products, on_device(): lax.dot_general(in_columns.reshape(groups, rows_total, in_columns.shape[1...  23.4 us
    all_gather x1, blocking collectives, on_device(): all_grads = lax.all_gather(gate_grad, 'dp', axis=0, tiled=True)  23.1 us
    all_to_all x1, blocking collectives, on_device(): lax.all_to_all(partial_value.astype(jnp.bfloat16), 'dp', split_axis=0, co...  9.09 us
    dot_general x1, matrix products, on_device(): lax.dot_general(all_grads, gate_local, contract_cols, preferred_element_t...  8.04 us
    all_gather x1, blocking collectives, on_device(): gathered_in = lax.all_gather(tokens_in, 'tp', axis=0, tiled=True)  4.93 us
    all_to_all x1, waiting for transfers between devices, on_device(): lax.all_to_all(gathered_in, 'dp', split_axis=1, concat_axis=0, tiled=True)  4.06 us
    all_to_all x1, starting transfers between devices, on_device(): lax.all_to_all(gathered_in, 'dp', split_axis=1, concat_axis=0, tiled=True)  3.32 us
  transfers between devices with their start and end apart: 3, of which 2 were waited for; matrix products, arithmetic and copies ran while one was open for 42% of the time, Pallas kernels for 0%

commit v1 on v0

v1 whole, which is shorter than its diff:
```python
import jax
import jax.numpy as jnp
from jax import lax
from jax.sharding import PartitionSpec as P


def to_behind(block, axis):
    size = lax.axis_size(axis)
    return lax.ppermute(block, axis, [(i, i - 1) for i in range(1, size)])


def rotated(blocks, start):
    size = blocks.shape[0]
    return lax.dynamic_slice_in_dim(jnp.concatenate([blocks, blocks]), start, size)


def gather_slots(block, axis):
    size = lax.axis_size(axis)
    z = lax.axis_index(axis)
    if size != 4:
        return rotated(lax.all_gather(block, axis), z)
    opposite = lax.ppermute(block, axis, [(i, (i + 2) % 4) for i in range(4)])
    from_low = lax.ppermute(block, axis, [(i, i + 1) for i in range(3)])
    from_high = lax.ppermute(block, axis, [(i + 1, i) for i in range(3)])
    ends = lax.ppermute(opposite, axis, [(2, 3), (1, 0)])
    after = jnp.where(z == 3, ends, from_high)
    before = jnp.where(z == 0, ends, from_low)
    return jnp.stack([block, after, opposite, before])


def on_device(layer_input, gate_pre, up_pre, hidden_grad, gate_weight):
    tokens_in = layer_input[0, 0]
    gate_val = gate_pre[0, 0].astype(jnp.float32)
    up_val = up_pre[0, 0].astype(jnp.float32)
    hidden_val = hidden_grad[0, 0].astype(jnp.float32)
    weight_t = gate_weight[0].T
    dp = lax.axis_size("dp")
    tp = lax.axis_size("tp")
    z = lax.axis_index("dp")
    own, width = tokens_in.shape
    block = width // dp
    tokens = own * tp
    hidden = weight_t.shape[0]
    logistic = jax.nn.sigmoid(gate_val)
    gate_grad = (hidden_val * up_val * logistic * (1.0 + gate_val * (1.0 - logistic))).astype(
        jnp.bfloat16
    )
    grads = gather_slots(gate_grad, "dp").reshape(dp * tokens, hidden)
    split_in = tokens_in.reshape(own, dp, block).transpose(1, 0, 2)
    sent_in = jnp.broadcast_to(split_in[None], (tp, dp, own, block))
    got_in = lax.all_to_all(sent_in.reshape(tp * dp, own, block), ("tp", "dp"), 0, 0, tiled=True)
    got_in = got_in.reshape(tp, dp, own, block).transpose(1, 0, 2, 3).reshape(dp, tokens, block)
    slots_in = rotated(got_in, z).reshape(dp * tokens, block)
    partial_value = jnp.dot(grads, weight_t, preferred_element_type=jnp.float32).astype(jnp.bfloat16)
    by_replica = rotated(partial_value.reshape(dp, tokens, block), (dp - z) % dp)
    to_owner = by_replica.reshape(dp, tp, own, block).transpose(1, 0, 2, 3)
    returned = lax.all_to_all(to_owner.reshape(tp * dp, own, block), ("tp", "dp"), 0, 0, tiled=True)
    summed = jnp.sum(returned.reshape(tp, dp, own, block).astype(jnp.float32), axis=0)
    input_grad = summed.astype(jnp.bfloat16).transpose(1, 0, 2).reshape(own, width)
    passed = to_behind(input_grad, "pp")
    weight_grad_t = lax.dot_general(
        grads, slots_in, (((0,), (0,)), ((), ())), preferred_element_type=jnp.float32
    ).astype(jnp.bfloat16)
    return (passed[None, None], weight_grad_t.T[None])


def solution(mesh):
    return jax.shard_map(
        on_device,
        mesh=mesh,
        in_specs=(
            P("pp", "dp", "tp", None),
            P("pp", "dp", None, "tp"),
            P("pp", "dp", None, "tp"),
            P("pp", "dp", None, "tp"),
            P("pp", "dp", "tp"),
        ),
        out_specs=(P("pp", "dp", "tp", None), P("pp", "dp", "tp")),
        check_vma=False,
    )
```

time: 124 us -> 60.6 us (0.49)
  the two profiles are of different devices: /device:TPU:0 before, /device:TPU:1 now
where the time goes in v1:
time: 60.6 us; the launch traced here: 60.1 us
  starting transfers between devices  20.7 us (34%)
  waiting for transfers between devices  16.9 us (28%)
  matrix products  15.9 us (26%)
  other arithmetic  3.04 us (5%)
  local copies, waits for them, and re-layouts  2.81 us (5%)
  between operations  0.74 us (1%)
    dot_general x1, matrix products, on_device(): jnp.dot(grads, weight_t, preferred_element_type=jnp.float32)  8.09 us
    dot_general x1, matrix products, on_device(): lax.dot_general(grads, slots_in, (((0,), (0,)), ((), ())), preferred_elem...  7.8 us
    ppermute x1, waiting for transfers between devices, gather_slots(): ends = lax.ppermute(opposite, axis, [(2, 3), (1, 0)])  6.85 us
    all_to_all x1, waiting for transfers between devices, on_device(): lax.all_to_all(to_owner.reshape(tp * dp, own, block), ('tp', 'dp'), 0, 0,...  6.34 us
    all_to_all x1, starting transfers between devices, on_device(): lax.all_to_all(sent_in.reshape(tp * dp, own, block), ('tp', 'dp'), 0, 0,...  4.31 us
    ppermute x1, starting transfers between devices, to_behind(): return lax.ppermute(block, axis, [(i, i - 1) for i in range(1, size)])  4 us
    ppermute x1, waiting for transfers between devices, gather_slots(): from_high = lax.ppermute(block, axis, [(i + 1, i) for i in range(3)])  3.44 us
    all_to_all x1, starting transfers between devices, on_device(): lax.all_to_all(to_owner.reshape(tp * dp, own, block), ('tp', 'dp'), 0, 0,...  3.37 us
  transfers between devices with their start and end apart: 7, of which 4 were waited for; matrix products, arithmetic and copies ran while one was open for 33% of the time, Pallas kernels for 0%

profile of v1, /device:TPU:1, one launch (start us, length us, event | category | flops | bytes accessed | tf_op | source)
XLA Modules:
  0.0 60.1 jit_solution(16100195193135535889)
XLA Ops:
  0.6 1.4 %fusion.15 = bf16[16,7392]{1,0:T(8,128)(2,1)S(1)} fusion(bf16[1,1,16,7392]{3,2,1,0:T(8,128)(2,1)} %param.6, bf16[1,1,16,7392]{3,2,1,0:T(8,128)(2,1)} %param.7, bf16[1,1,16,7392]{3,2,1,0:T(8,128)(2,1)} %param.8), kind=kLoop, calls=%fused_computation.17 | loop fusion | flops 1537536 | bytes 946176 | tf_op jit(solution)/shard_map/convert_element_type | solution.py:45
  2.0 3.2 %collective-permute-start = (bf16[16,7392]{1,0:T(8,128)(2,1)S(1)}, bf16[16,7392]{1,0:T(8,128)(2,1)S(1)}, u32[]{:S(2)}, u32[]{:S(2)}) collective-permute-start(bf16[16,7392]{1,0:T(8,128)(2,1)S(1)} %fusion.15), channel_id=1, source_target_pairs={{0,2},{1,3},{2,0},{3,1},{4,6},{5,7},{6,4},{7,5},{8,10},{9,11},{10,... | collective-permute-start | bytes 709640 | tf_op jit(solution)/shard_map/ppermute | solution.py:22
  5.2 3.2 %collective-permute-start.3 = (bf16[16,7392]{1,0:T(8,128)(2,1)S(1)}, bf16[16,7392]{1,0:T(8,128)(2,1)S(1)}, u32[]{:S(2)}, u32[]{:S(2)}) collective-permute-start(bf16[16,7392]{1,0:T(8,128)(2,1)S(1)} %fusion.15), channel_id=1, source_target_pairs={{0,1},{1,2},{2,3},{4,5},{5,6},{6,7},{8,9},{9,10},{10,11},{12,13},{... | collective-permute-start | bytes 709640 | tf_op jit(solution)/shard_map/ppermute | solution.py:23
  8.4 1.3 %collective-permute-start.2 = (bf16[16,7392]{1,0:T(8,128)(2,1)S(1)}, bf16[16,7392]{1,0:T(8,128)(2,1)S(1)}, u32[]{:S(2)}, u32[]{:S(2)}) collective-permute-start(bf16[16,7392]{1,0:T(8,128)(2,1)S(1)} %fusion.15), channel_id=1, source_target_pairs={{1,0},{2,1},{3,2},{5,4},{6,5},{7,6},{9,8},{10,9},{11,10},{13,12},{... | collective-permute-start | bytes 709640 | tf_op jit(solution)/shard_map/ppermute | solution.py:24
  9.7 1.5 %broadcast_in_dim.13 = bf16[2,4,8,1024]{3,2,1,0:T(8,128)(2,1)} broadcast(bf16[4,8,1024]{2,1,0:T(8,128)(2,1)} %bitcast.94), dimensions={1,2,3} | broadcast | bytes 196608 | tf_op jit(solution)/shard_map/broadcast_in_dim | solution.py:50
  11.2 4.3 %all-to-all-start.1 = ((bf16[8,8,1024]{2,1,0:T(8,128)(2,1)}), bf16[8,8,1024]{2,1,0:T(8,128)(2,1)S(1)}, u32[]{:S(2)}, u32[]{:S(2)}) async-start(bf16[8,8,1024]{2,1,0:T(8,128)(2,1)} %bitcast.19), calls=%async_computation.1 | async-start | bytes 262144 | tf_op jit(solution)/shard_map/all_to_all | solution.py:51
  15.5 0.3 collective-permute-done
  15.8 1.3 %collective-permute-start.1 = (bf16[16,7392]{1,0:T(8,128)(2,1)S(1)}, bf16[16,7392]{1,0:T(8,128)(2,1)S(1)}, u32[]{:S(2)}, u32[]{:S(2)}) collective-permute-start(bf16[16,7392]{1,0:T(8,128)(2,1)S(1)} %collective-permute-done), channel_id=1, source_target_pairs={{2,3},{1,0},{6,7},{5,4},{10,11},{9,8},{14,15},{13,12},{18,19},{17,... | collective-permute-start | bytes 709640 | tf_op jit(solution)/shard_map/ppermute | solution.py:25
  17.1 1.4 %fusion.21 = bf16[1,16,7392]{2,1,0:T(8,128)(2,1)S(1)} fusion(bf16[1,1,16,7392]{3,2,1,0:T(8,128)(2,1)} %param.6, bf16[1,1,16,7392]{3,2,1,0:T(8,128)(2,1)} %param.7, bf16[1,1,16,7392]{3,2,1,0:T(8,128)(2,1)} %param.8), kind=kLoop, calls=%fused_computation.23 | loop fusion | flops 1537536 | bytes 946176 | tf_op jit(solution)/shard_map/convert_element_type | solution.py:45
  18.5 0.0 collective-permute-done.3
  18.5 3.4 %collective-permute-done.2 = bf16[16,7392]{1,0:T(8,128)(2,1)S(1)} collective-permute-done((bf16[16,7392]{1,0:T(8,128)(2,1)S(1)}, bf16[16,7392]{1,0:T(8,128)(2,1)S(1)}, u32[]{:S(2)}, u32[]{:S(2)}) %collective-permute-start.2) | collective-permute-done | bytes 236576 | tf_op jit(solution)/shard_map/ppermute | solution.py:24
  22.0 6.8 %collective-permute-done.1 = bf16[16,7392]{1,0:T(8,128)(2,1)S(1)} collective-permute-done((bf16[16,7392]{1,0:T(8,128)(2,1)S(1)}, bf16[16,7392]{1,0:T(8,128)(2,1)S(1)}, u32[]{:S(2)}, u32[]{:S(2)}) %collective-permute-start.1) | collective-permute-done | bytes 236576 | tf_op jit(solution)/shard_map/ppermute | solution.py:25
  28.9 0.1 pad_maximum_fusion
  29.0 8.1 %fusion.3 = bf16[64,1024]{1,0:T(8,128)(2,1)S(1)} fusion(bf16[64,7392]{1,0:T(8,128)(2,1)S(1)} %bitcast.87, bf16[1,1024,7392]{1,2,0:T(8,128)(2,1)} %param.9), kind=kOutput, calls=%fused_computation.4 | convolution fusion | flops 968949760 | bytes 16216064 | tf_op jit(solution)/shard_map/dot_general | solution.py:54
  37.1 0.1 fusion.25
  37.2 0.7 %copy.8 = bf16[2,4,8,1024]{3,2,1,0:T(8,128)(2,1)} copy(bf16[2,4,8,1024]{3,2,0,1:T(8,128)(2,1)S(1)} %fusion.25) | data formatting | bytes 262144 | tf_op jit(solution)/shard_map/transpose | solution.py:56
  37.9 0.0 all-to-all-done.1
  37.9 3.4 %all-to-all-start = ((bf16[8,8,1024]{2,1,0:T(8,128)(2,1)}), bf16[8,8,1024]{2,1,0:T(8,128)(2,1)S(1)}, u32[]{:S(2)}, u32[]{:S(2)}) async-start(bf16[8,8,1024]{2,1,0:T(8,128)(2,1)} %bitcast.12), calls=%async_computation | async-start | bytes 262144 | tf_op jit(solution)/shard_map/all_to_all | solution.py:57
  41.3 6.3 %all-to-all-done = bf16[8,8,1024]{2,1,0:T(8,128)(2,1)S(1)} async-done(((bf16[8,8,1024]{2,1,0:T(8,128)(2,1)}), bf16[8,8,1024]{2,1,0:T(8,128)(2,1)S(1)}, u32[]{:S(2)}, u32[]{:S(2)}) %all-to-all-start) | async-done | bytes 131104 | tf_op jit(solution)/shard_map/all_to_all | solution.py:57
  47.6 4.0 %collective-permute-start.4 = (bf16[8,4096]{1,0:T(8,128)(2,1)S(1)}, bf16[8,4096]{1,0:T(8,128)(2,1)S(1)}, u32[]{:S(2)}, u32[]{:S(2)}) collective-permute-start(bf16[8,4096]{1,0:T(8,128)(2,1)S(1)} %bitcast.95), channel_id=1, source_target_pairs={{8,0},{16,8},{24,16},{9,1},{17,9},{25,17},{10,2},{18,10},{26,18},{... | collective-permute-start | bytes 196616 | tf_op jit(solution)/shard_map/ppermute | solution.py:9
  51.6 7.8 %fusion.2 = bf16[1,1024,7392]{1,2,0:T(8,128)(2,1)} fusion(s32[]{:T(128)S(6)} %select_n.33, bf16[4,16,1024]{2,1,0:T(8,128)(2,1)S(1)} %bitcast.90, bf16[1,16,7392]{2,1,0:T(8,128)(2,1)S(1)} %get-tuple-element.3, bf16[1,16,7392]{2,1,0:T(8,128)(2,1)S(1)} %bitcast.89, bf16[1,16,7392]{2,1,0:T(8,128)(2,1)S(1)} %get-tuple-element.2, bf16[1,16,7392]{2,1,0:T(8,128)(2,1)S(1)} %fusion.21), kind=kOutput, calls=%fused_computation.3 | convolution fusion | flops 977938432 | bytes 16216068 | tf_op jit(solution)/shard_map/dot_general | solution.py:61
  59.4 0.0 collective-permute-done.4
  59.4 0.6 %copy.13 = bf16[1,1,8,4096]{3,2,1,0:T(8,128)(2,1)} copy(bf16[1,1,8,4096]{3,2,1,0:T(8,128)(2,1)S(1)} %bitcast.96) | data formatting | bytes 131072
  (3 shorter events, 0.1 us)
Async XLA Ops:
  2.0 13.8 %collective-permute-start = (bf16[16,7392]{1,0:T(8,128)(2,1)S(1)}, bf16[16,7392]{1,0:T(8,128)(2,1)S(1)}, u32[]{:S(2)}, u32[]{:S(2)}) collective-permute-start(bf16[16,7392]{1,0:T(8,128)(2,1)S(1)} %fusion.15), channel_id=1, source_target_pairs={{0,2},{1,3},{2,0},{3,1},{4,6},{5,7},{6,4},{7,5},{8,10},{9,11},{10,... | collective-permute-start | bytes 709640 | tf_op jit(solution)/shard_map/ppermute | solution.py:22
  5.2 13.3 %collective-permute-start.3 = (bf16[16,7392]{1,0:T(8,128)(2,1)S(1)}, bf16[16,7392]{1,0:T(8,128)(2,1)S(1)}, u32[]{:S(2)}, u32[]{:S(2)}) collective-permute-start(bf16[16,7392]{1,0:T(8,128)(2,1)S(1)} %fusion.15), channel_id=1, source_target_pairs={{0,1},{1,2},{2,3},{4,5},{5,6},{6,7},{8,9},{9,10},{10,11},{12,13},{... | collective-permute-start | bytes 709640 | tf_op jit(solution)/shard_map/ppermute | solution.py:23
  8.4 13.6 %collective-permute-start.2 = (bf16[16,7392]{1,0:T(8,128)(2,1)S(1)}, bf16[16,7392]{1,0:T(8,128)(2,1)S(1)}, u32[]{:S(2)}, u32[]{:S(2)}) collective-permute-start(bf16[16,7392]{1,0:T(8,128)(2,1)S(1)} %fusion.15), channel_id=1, source_target_pairs={{1,0},{2,1},{3,2},{5,4},{6,5},{7,6},{9,8},{10,9},{11,10},{13,12},{... | collective-permute-start | bytes 709640 | tf_op jit(solution)/shard_map/ppermute | solution.py:24
  11.2 26.6 %all-to-all-start.1 = ((bf16[8,8,1024]{2,1,0:T(8,128)(2,1)}), bf16[8,8,1024]{2,1,0:T(8,128)(2,1)S(1)}, u32[]{:S(2)}, u32[]{:S(2)}) async-start(bf16[8,8,1024]{2,1,0:T(8,128)(2,1)} %bitcast.19), calls=%async_computation.1 | async-start | bytes 262144 | tf_op jit(solution)/shard_map/all_to_all | solution.py:51
  15.8 13.0 %collective-permute-start.1 = (bf16[16,7392]{1,0:T(8,128)(2,1)S(1)}, bf16[16,7392]{1,0:T(8,128)(2,1)S(1)}, u32[]{:S(2)}, u32[]{:S(2)}) collective-permute-start(bf16[16,7392]{1,0:T(8,128)(2,1)S(1)} %collective-permute-done), channel_id=1, source_target_pairs={{2,3},{1,0},{6,7},{5,4},{10,11},{9,8},{14,15},{13,12},{18,19},{17,... | collective-permute-start | bytes 709640 | tf_op jit(solution)/shard_map/ppermute | solution.py:25
  37.9 9.7 %all-to-all-start = ((bf16[8,8,1024]{2,1,0:T(8,128)(2,1)}), bf16[8,8,1024]{2,1,0:T(8,128)(2,1)S(1)}, u32[]{:S(2)}, u32[]{:S(2)}) async-start(bf16[8,8,1024]{2,1,0:T(8,128)(2,1)} %bitcast.12), calls=%async_computation | async-start | bytes 262144 | tf_op jit(solution)/shard_map/all_to_all | solution.py:57
  47.6 11.8 %collective-permute-start.4 = (bf16[8,4096]{1,0:T(8,128)(2,1)S(1)}, bf16[8,4096]{1,0:T(8,128)(2,1)S(1)}, u32[]{:S(2)}, u32[]{:S(2)}) collective-permute-start(bf16[8,4096]{1,0:T(8,128)(2,1)S(1)} %bitcast.95), channel_id=1, source_target_pairs={{8,0},{16,8},{24,16},{9,1},{17,9},{25,17},{10,2},{18,10},{26,18},{... | collective-permute-start | bytes 196616 | tf_op jit(solution)/shard_map/ppermute | solution.py:9

commit v2 on v1

--- a/solution.py
+++ b/solution.py
@@ -55,12 +55,13 @@
     by_replica = rotated(partial_value.reshape(dp, tokens, block), (dp - z) % dp)
     to_owner = by_replica.reshape(dp, tp, own, block).transpose(1, 0, 2, 3)
     returned = lax.all_to_all(to_owner.reshape(tp * dp, own, block), ("tp", "dp"), 0, 0, tiled=True)
+    weight_grad_t = lax.dot_general(
+        grads, slots_in, (((0,), (0,)), ((), ())), preferred_element_type=jnp.float32
+    ).astype(jnp.bfloat16)
+    returned, weight_grad_t = lax.optimization_barrier((returned, weight_grad_t))
     summed = jnp.sum(returned.reshape(tp, dp, own, block).astype(jnp.float32), axis=0)
     input_grad = summed.astype(jnp.bfloat16).transpose(1, 0, 2).reshape(own, width)
     passed = to_behind(input_grad, "pp")
-    weight_grad_t = lax.dot_general(
-        grads, slots_in, (((0,), (0,)), ((), ())), preferred_element_type=jnp.float32
-    ).astype(jnp.bfloat16)
     return (passed[None, None], weight_grad_t.T[None])
 
 

time: 60.6 us -> 56.1 us (0.926)
  waiting for transfers between devices: 16.9 us -> 13.6 us
  starting transfers between devices: 20.7 us -> 19.5 us
    all_to_all x1, waiting for transfers between devices: 6.34 us -> 0.01 us  [on_device(): lax.all_to_all(to_owner.reshape(tp * dp, own, block), ('tp', 'dp'), 0, 0,...]
    all_to_all x1, waiting for transfers between devices: 0.01 us -> 5.51 us  [on_device(): lax.all_to_all(sent_in.reshape(tp * dp, own, block), ('tp', 'dp'), 0, 0,...]
    ppermute x1, waiting for transfers between devices: 3.44 us -> 0.01 us  [gather_slots(): from_high = lax.ppermute(block, axis, [(i + 1, i) for i in range(3)])]
    ppermute x1, waiting for transfers between devices: 0.01 us -> 3.03 us  [to_behind(): return lax.ppermute(block, axis, [(i, i - 1) for i in range(1, size)])]
    ppermute x1, waiting for transfers between devices: 6.85 us -> 4.75 us  [gather_slots(): ends = lax.ppermute(opposite, axis, [(2, 3), (1, 0)])]
    ppermute x1, starting transfers between devices: 4 us -> 2.83 us  [to_behind(): return lax.ppermute(block, axis, [(i, i - 1) for i in range(1, size)])]
  transfers between devices with their start and end apart: 7 -> 7, of which waited for: 4 -> 4; matrix products, arithmetic and copies ran while one was open for 33% -> 19% of each run, Pallas kernels for 0% -> 0%
where the time goes in v2:
time: 56.1 us; the launch traced here: 55.6 us
  starting transfers between devices  19.5 us (35%)
  matrix products  15.9 us (28%)
  waiting for transfers between devices  13.6 us (24%)
  other arithmetic  3.04 us (5%)
  local copies, waits for them, and re-layouts  2.81 us (5%)
  between operations  0.75 us (1%)
    dot_general x1, matrix products, on_device(): jnp.dot(grads, weight_t, preferred_element_type=jnp.float32)  8.09 us
    dot_general x1, matrix products, on_device(): lax.dot_general(grads, slots_in, (((0,), (0,)), ((), ())), preferred_elem...  7.8 us
    all_to_all x1, waiting for transfers between devices, on_device(): lax.all_to_all(sent_in.reshape(tp * dp, own, block), ('tp', 'dp'), 0, 0,...  5.51 us
    ppermute x1, waiting for transfers between devices, gather_slots(): ends = lax.ppermute(opposite, axis, [(2, 3), (1, 0)])  4.75 us
    all_to_all x1, starting transfers between devices, on_device(): lax.all_to_all(sent_in.reshape(tp * dp, own, block), ('tp', 'dp'), 0, 0,...  4.31 us
    all_to_all x1, starting transfers between devices, on_device(): lax.all_to_all(to_owner.reshape(tp * dp, own, block), ('tp', 'dp'), 0, 0,...  3.37 us
    ppermute x1, starting transfers between devices, gather_slots(): from_low = lax.ppermute(block, axis, [(i, i + 1) for i in range(3)])  3.2 us
    ppermute x1, starting transfers between devices, gather_slots(): opposite = lax.ppermute(block, axis, [(i, (i + 2) % 4) for i in range(4)])  3.19 us
  transfers between devices with their start and end apart: 7, of which 4 were waited for; matrix products, arithmetic and copies ran while one was open for 19% of the time, Pallas kernels for 0%

profile of v2, /device:TPU:1, one launch (start us, length us, event | category | flops | bytes accessed | tf_op | source)
XLA Modules:
  0.0 55.6 jit_solution(5239928763379309625)
XLA Ops:
  0.6 1.4 %fusion.14 = bf16[16,7392]{1,0:T(8,128)(2,1)S(1)} fusion(bf16[1,1,16,7392]{3,2,1,0:T(8,128)(2,1)} %param.6, bf16[1,1,16,7392]{3,2,1,0:T(8,128)(2,1)} %param.7, bf16[1,1,16,7392]{3,2,1,0:T(8,128)(2,1)} %param.8), kind=kLoop, calls=%fused_computation.16 | loop fusion | flops 1537536 | bytes 946176 | tf_op jit(solution)/shard_map/convert_element_type | solution.py:45
  2.0 3.2 %collective-permute-start = (bf16[16,7392]{1,0:T(8,128)(2,1)S(1)}, bf16[16,7392]{1,0:T(8,128)(2,1)S(1)}, u32[]{:S(2)}, u32[]{:S(2)}) collective-permute-start(bf16[16,7392]{1,0:T(8,128)(2,1)S(1)} %fusion.14), channel_id=1, source_target_pairs={{0,2},{1,3},{2,0},{3,1},{4,6},{5,7},{6,4},{7,5},{8,10},{9,11},{10,... | collective-permute-start | bytes 709640 | tf_op jit(solution)/shard_map/ppermute | solution.py:22
  5.2 3.2 %collective-permute-start.3 = (bf16[16,7392]{1,0:T(8,128)(2,1)S(1)}, bf16[16,7392]{1,0:T(8,128)(2,1)S(1)}, u32[]{:S(2)}, u32[]{:S(2)}) collective-permute-start(bf16[16,7392]{1,0:T(8,128)(2,1)S(1)} %fusion.14), channel_id=1, source_target_pairs={{0,1},{1,2},{2,3},{4,5},{5,6},{6,7},{8,9},{9,10},{10,11},{12,13},{... | collective-permute-start | bytes 709640 | tf_op jit(solution)/shard_map/ppermute | solution.py:23
  8.4 1.3 %collective-permute-start.2 = (bf16[16,7392]{1,0:T(8,128)(2,1)S(1)}, bf16[16,7392]{1,0:T(8,128)(2,1)S(1)}, u32[]{:S(2)}, u32[]{:S(2)}) collective-permute-start(bf16[16,7392]{1,0:T(8,128)(2,1)S(1)} %fusion.14), channel_id=1, source_target_pairs={{1,0},{2,1},{3,2},{5,4},{6,5},{7,6},{9,8},{10,9},{11,10},{13,12},{... | collective-permute-start | bytes 709640 | tf_op jit(solution)/shard_map/ppermute | solution.py:24
  9.7 1.5 %broadcast_in_dim.12 = bf16[2,4,8,1024]{3,2,1,0:T(8,128)(2,1)} broadcast(bf16[4,8,1024]{2,1,0:T(8,128)(2,1)} %bitcast.93), dimensions={1,2,3} | broadcast | bytes 196608 | tf_op jit(solution)/shard_map/broadcast_in_dim | solution.py:50
  11.2 4.3 %all-to-all-start.1 = ((bf16[8,8,1024]{2,1,0:T(8,128)(2,1)}), bf16[8,8,1024]{2,1,0:T(8,128)(2,1)S(1)}, u32[]{:S(2)}, u32[]{:S(2)}) async-start(bf16[8,8,1024]{2,1,0:T(8,128)(2,1)} %bitcast.15), calls=%async_computation.1 | async-start | bytes 262144 | tf_op jit(solution)/shard_map/all_to_all | solution.py:51
  15.5 0.3 collective-permute-done
  15.8 1.3 %collective-permute-start.1 = (bf16[16,7392]{1,0:T(8,128)(2,1)S(1)}, bf16[16,7392]{1,0:T(8,128)(2,1)S(1)}, u32[]{:S(2)}, u32[]{:S(2)}) collective-permute-start(bf16[16,7392]{1,0:T(8,128)(2,1)S(1)} %collective-permute-done), channel_id=1, source_target_pairs={{2,3},{1,0},{6,7},{5,4},{10,11},{9,8},{14,15},{13,12},{18,19},{17,... | collective-permute-start | bytes 709640 | tf_op jit(solution)/shard_map/ppermute | solution.py:25
  17.1 1.4 %fusion.20 = bf16[1,16,7392]{2,1,0:T(8,128)(2,1)S(1)} fusion(bf16[1,1,16,7392]{3,2,1,0:T(8,128)(2,1)} %param.6, bf16[1,1,16,7392]{3,2,1,0:T(8,128)(2,1)} %param.7, bf16[1,1,16,7392]{3,2,1,0:T(8,128)(2,1)} %param.8), kind=kLoop, calls=%fused_computation.22 | loop fusion | flops 1537536 | bytes 946176 | tf_op jit(solution)/shard_map/convert_element_type | solution.py:45
  18.5 5.5 %all-to-all-done.1 = bf16[8,8,1024]{2,1,0:T(8,128)(2,1)S(1)} async-done(((bf16[8,8,1024]{2,1,0:T(8,128)(2,1)}), bf16[8,8,1024]{2,1,0:T(8,128)(2,1)S(1)}, u32[]{:S(2)}, u32[]{:S(2)}) %all-to-all-start.1) | async-done | bytes 131104 | tf_op jit(solution)/shard_map/all_to_all | solution.py:51
  24.1 0.0 collective-permute-done.3
  24.1 0.0 collective-permute-done.2
  24.1 4.8 %collective-permute-done.1 = bf16[16,7392]{1,0:T(8,128)(2,1)S(1)} collective-permute-done((bf16[16,7392]{1,0:T(8,128)(2,1)S(1)}, bf16[16,7392]{1,0:T(8,128)(2,1)S(1)}, u32[]{:S(2)}, u32[]{:S(2)}) %collective-permute-start.1) | collective-permute-done | bytes 236576 | tf_op jit(solution)/shard_map/ppermute | solution.py:25
  28.9 0.1 pad_maximum_fusion
  29.0 8.1 %fusion.2 = bf16[64,1024]{1,0:T(8,128)(2,1)S(1)} fusion(bf16[64,7392]{1,0:T(8,128)(2,1)S(1)} %bitcast.86, bf16[1,1024,7392]{1,2,0:T(8,128)(2,1)} %param.9), kind=kOutput, calls=%fused_computation.3 | convolution fusion | flops 968949760 | bytes 16216064 | tf_op jit(solution)/shard_map/dot_general | solution.py:54
  37.1 0.1 fusion.24
  37.2 0.7 %copy.8 = bf16[2,4,8,1024]{3,2,1,0:T(8,128)(2,1)} copy(bf16[2,4,8,1024]{3,2,0,1:T(8,128)(2,1)S(1)} %fusion.24) | data formatting | bytes 262144 | tf_op jit(solution)/shard_map/transpose | solution.py:56
  37.8 3.4 %all-to-all-start = ((bf16[8,8,1024]{2,1,0:T(8,128)(2,1)}), bf16[8,8,1024]{2,1,0:T(8,128)(2,1)S(1)}, u32[]{:S(2)}, u32[]{:S(2)}) async-start(bf16[8,8,1024]{2,1,0:T(8,128)(2,1)} %bitcast.12), calls=%async_computation | async-start | bytes 262144 | tf_op jit(solution)/shard_map/all_to_all | solution.py:57
  41.2 7.8 %bitcast_convert_fusion = bf16[7392,1024]{1,0:T(8,128)(2,1)} fusion(s32[]{:T(128)S(6)} %select_n.33, bf16[4,16,1024]{2,1,0:T(8,128)(2,1)S(1)} %bitcast.92, bf16[1,16,7392]{2,1,0:T(8,128)(2,1)S(1)} %get-tuple-element.7, bf16[1,16,7392]{2,1,0:T(8,128)(2,1)S(1)} %bitcast.91, bf16[1,16,7392]{2,1,0:T(8,128)(2,1)S(1)} %get-tuple-element.6, ...), kind=kOutput, calls=%fused_computation | convolution fusion | flops 977938432 | bytes 16216068 | tf_op jit(solution)/shard_map/dot_general | solution.py:58
  49.0 0.0 all-to-all-done
  49.1 2.8 %collective-permute-start.4 = (bf16[8,4096]{1,0:T(8,128)(2,1)S(1)}, bf16[8,4096]{1,0:T(8,128)(2,1)S(1)}, u32[]{:S(2)}, u32[]{:S(2)}) collective-permute-start(bf16[8,4096]{1,0:T(8,128)(2,1)S(1)} %bitcast.94), channel_id=1, source_target_pairs={{8,0},{16,8},{24,16},{9,1},{17,9},{25,17},{10,2},{18,10},{26,18},{... | collective-permute-start | bytes 196616 | tf_op jit(solution)/shard_map/ppermute | solution.py:9
  51.9 3.0 %collective-permute-done.4 = bf16[8,4096]{1,0:T(8,128)(2,1)S(1)} collective-permute-done((bf16[8,4096]{1,0:T(8,128)(2,1)S(1)}, bf16[8,4096]{1,0:T(8,128)(2,1)S(1)}, u32[]{:S(2)}, u32[]{:S(2)}) %collective-permute-start.4) | collective-permute-done | bytes 65568 | tf_op jit(solution)/shard_map/ppermute | solution.py:9
  54.9 0.6 %copy.13 = bf16[1,1,8,4096]{3,2,1,0:T(8,128)(2,1)} copy(bf16[1,1,8,4096]{3,2,1,0:T(8,128)(2,1)S(1)} %bitcast.95) | data formatting | bytes 131072
  (3 shorter events, 0.1 us)
Async XLA Ops:
  2.0 13.8 %collective-permute-start = (bf16[16,7392]{1,0:T(8,128)(2,1)S(1)}, bf16[16,7392]{1,0:T(8,128)(2,1)S(1)}, u32[]{:S(2)}, u32[]{:S(2)}) collective-permute-start(bf16[16,7392]{1,0:T(8,128)(2,1)S(1)} %fusion.14), channel_id=1, source_target_pairs={{0,2},{1,3},{2,0},{3,1},{4,6},{5,7},{6,4},{7,5},{8,10},{9,11},{10,... | collective-permute-start | bytes 709640 | tf_op jit(solution)/shard_map/ppermute | solution.py:22
  5.2 18.8 %collective-permute-start.3 = (bf16[16,7392]{1,0:T(8,128)(2,1)S(1)}, bf16[16,7392]{1,0:T(8,128)(2,1)S(1)}, u32[]{:S(2)}, u32[]{:S(2)}) collective-permute-start(bf16[16,7392]{1,0:T(8,128)(2,1)S(1)} %fusion.14), channel_id=1, source_target_pairs={{0,1},{1,2},{2,3},{4,5},{5,6},{6,7},{8,9},{9,10},{10,11},{12,13},{... | collective-permute-start | bytes 709640 | tf_op jit(solution)/shard_map/ppermute | solution.py:23
  8.4 15.6 %collective-permute-start.2 = (bf16[16,7392]{1,0:T(8,128)(2,1)S(1)}, bf16[16,7392]{1,0:T(8,128)(2,1)S(1)}, u32[]{:S(2)}, u32[]{:S(2)}) collective-permute-start(bf16[16,7392]{1,0:T(8,128)(2,1)S(1)} %fusion.14), channel_id=1, source_target_pairs={{1,0},{2,1},{3,2},{5,4},{6,5},{7,6},{9,8},{10,9},{11,10},{13,12},{... | collective-permute-start | bytes 709640 | tf_op jit(solution)/shard_map/ppermute | solution.py:24
  11.2 12.8 %all-to-all-start.1 = ((bf16[8,8,1024]{2,1,0:T(8,128)(2,1)}), bf16[8,8,1024]{2,1,0:T(8,128)(2,1)S(1)}, u32[]{:S(2)}, u32[]{:S(2)}) async-start(bf16[8,8,1024]{2,1,0:T(8,128)(2,1)} %bitcast.15), calls=%async_computation.1 | async-start | bytes 262144 | tf_op jit(solution)/shard_map/all_to_all | solution.py:51
  15.8 13.0 %collective-permute-start.1 = (bf16[16,7392]{1,0:T(8,128)(2,1)S(1)}, bf16[16,7392]{1,0:T(8,128)(2,1)S(1)}, u32[]{:S(2)}, u32[]{:S(2)}) collective-permute-start(bf16[16,7392]{1,0:T(8,128)(2,1)S(1)} %collective-permute-done), channel_id=1, source_target_pairs={{2,3},{1,0},{6,7},{5,4},{10,11},{9,8},{14,15},{13,12},{18,19},{17,... | collective-permute-start | bytes 709640 | tf_op jit(solution)/shard_map/ppermute | solution.py:25
  37.8 11.2 %all-to-all-start = ((bf16[8,8,1024]{2,1,0:T(8,128)(2,1)}), bf16[8,8,1024]{2,1,0:T(8,128)(2,1)S(1)}, u32[]{:S(2)}, u32[]{:S(2)}) async-start(bf16[8,8,1024]{2,1,0:T(8,128)(2,1)} %bitcast.12), calls=%async_computation | async-start | bytes 262144 | tf_op jit(solution)/shard_map/all_to_all | solution.py:57
  49.1 5.9 %collective-permute-start.4 = (bf16[8,4096]{1,0:T(8,128)(2,1)S(1)}, bf16[8,4096]{1,0:T(8,128)(2,1)S(1)}, u32[]{:S(2)}, u32[]{:S(2)}) collective-permute-start(bf16[8,4096]{1,0:T(8,128)(2,1)S(1)} %bitcast.94), channel_id=1, source_target_pairs={{8,0},{16,8},{24,16},{9,1},{17,9},{25,17},{10,2},{18,10},{26,18},{... | collective-permute-start | bytes 196616 | tf_op jit(solution)/shard_map/ppermute | solution.py:9
